TPU v7x, 32 devices: a whole 2x2x4 slice. The times are simulated.
32 devices in a mesh: group: 2 (over y), plane: 4 (over z), planey: 2 (over x), ens: 2 (over core).
Axes of the slice: x: 2, y: 2, z: 4, core: 2. Of those that a mesh axis runs over, the one named last changes fastest.
Arguments:
- u_prior: float32 [8, 2, 10, 64, 256], P(('group', 'ens'), None, None, 'plane', 'planey'), parts along dimension 0, may hold values from -6 to 6
- friction_rows: int32 [8], P(('group', 'ens')), parts along dimension 0, may hold values from 0 to 15
- friction_table: float32 [32, 64, 256], P('group', 'plane', 'planey'), parts along dimension 0, may hold values from 0.3 to 3
- bed_fixed: int32 [64, 256], P('plane', 'planey'), may hold values from -536870912 to 536870911
- ice_mask: int32 [64, 256], P('plane', 'planey'), may hold values 0 or 1
Outputs:
- mean_velocity: float32 [4, 10, 64, 256], P('group', None, 'plane', 'planey'), parts along dimension 0
There are 2 independent parts, one for each index of `group`. A program takes and returns all parts, laid end to end along the dimension named above; an argument that names none is the same for every part. Nothing has to cross between parts.
Inputs may be any that keep to these rules, and one draw needn't show every extreme that they name: `friction_rows`: each sample names one row of the friction table.
All inputs are finite; a program needn't handle non-finite values. No bound on the sum of `ice_mask` on one device may be relied on, other than what follows from the above.
Results may differ from a plain program's by a relative error of at most 0.0003.
Values sent between devices are 32-bit elements; how exact they have to be, the bound alone decides.
A program may use at most 64 MiB of HBM per device.

v0:
```python
import jax
import jax.numpy as jnp
from jax import lax
from jax.sharding import PartitionSpec as P

bed_unit = 2.0 ** (-29)
factor_u = (2.0, 1.0, 0.5)
factor_v = (2.0, 0.5, 1.0)


def extended_2(cells, sides, width):
    for axis, dim in sides:
        count = lax.axis_size(axis)
        ends = count - 1
        head = lax.slice_in_dim(cells, 0, width, axis=dim)
        tail = lax.slice_in_dim(cells, cells.shape[dim] - width, cells.shape[dim], axis=dim)
        cells = jnp.concatenate(
            [
                lax.ppermute(tail, axis, [(i, (i + 1) % count) for i in range(ends)]),
                cells,
                lax.ppermute(head, axis, [((i + 1) % count, i) for i in range(ends)]),
            ],
            axis=dim,
        )
    return cells


def coefficient(offset):
    nonzero = len([entry for entry in offset if entry != 0])
    weight_u = 0.25 ** (nonzero - 1)
    weight_v = weight_u
    for dimension in range(3):
        if offset[dimension] != 0:
            weight_u = weight_u * factor_u[dimension]
            weight_v = weight_v * factor_v[dimension]
    return jnp.array([weight_u, weight_v], jnp.float32).reshape(2, 1, 1, 1)


def neighbour_sum(padded):
    layers = padded.shape[-3] - 2
    span_x = padded.shape[-2] - 2
    span_y = padded.shape[-1] - 2
    summed = None
    for step_z in (-1, 0, 1):
        for step_x in (-1, 0, 1):
            for step_y in (-1, 0, 1):
                if step_z == 0 and step_x == 0 and (step_y == 0):
                    continue
                window = padded[
                    ...,
                    1 + step_z : 1 + step_z + layers,
                    1 + step_x : 1 + step_x + span_x,
                    1 + step_y : 1 + step_y + span_y,
                ]
                addend = coefficient((step_z, step_x, step_y)) * window
                summed = addend if summed is None else summed + addend
    return summed


def strain_roots(extended):
    padded = jnp.pad(extended, [(0, 0)] * (extended.ndim - 3) + [(1, 1), (0, 0), (0, 0)])
    along_x = (padded[..., 1:-1, 2:, 1:-1] - padded[..., 1:-1, :-2, 1:-1]) * 0.5
    along_y = (padded[..., 1:-1, 1:-1, 2:] - padded[..., 1:-1, 1:-1, :-2]) * 0.5
    along_z = (padded[..., 2:, 1:-1, 1:-1] - padded[..., :-2, 1:-1, 1:-1]) * 0.5
    stretch_x = along_x[..., 0, :, :, :]
    stretch_y = along_y[..., 1, :, :, :]
    shear_one = along_y[..., 0, :, :, :]
    shear_two = along_x[..., 1, :, :, :]
    vertical_u = along_z[..., 0, :, :, :]
    vertical_v = along_z[..., 1, :, :, :]
    shear = shear_one + shear_two
    strain = (
        stretch_x * stretch_x
        + stretch_y * stretch_y
        + stretch_x * stretch_y
        + 0.25 * shear * shear
        + 0.25 * (vertical_u * vertical_u + vertical_v * vertical_v)
    )
    return jnp.power(strain + 0.1, -1.0 / 6.0)[..., None, :, :, :]


def pad_layers(field):
    return jnp.pad(field, ((0, 0), (0, 0), (1, 1), (0, 0), (0, 0)))


def inner(left, right):
    return jnp.sum(left * right, axis=(1, 2, 3, 4))


def spread(values):
    return values.reshape(-1, 1, 1, 1, 1)


def trimmed(field, margin):
    return field[..., margin:-margin, margin:-margin]


def apply_local(roots_wide, across_part, diag_part, field_wide):
    product = roots_wide * field_wide
    nearby = neighbour_sum(pad_layers(product))
    centre = trimmed(field_wide, 1)
    return trimmed(roots_wide, 1) * (across_part * centre - nearby) + diag_part * centre


def body(u_prior, friction_rows, friction_table, bed_fixed, ice_mask):
    members = u_prior.shape[0]
    layers = u_prior.shape[2]
    rows_x = u_prior.shape[3]
    rows_y = u_prior.shape[4]
    total_x = rows_x * lax.axis_size("plane")
    cover = ice_mask.astype(jnp.float32)
    bed_block = (bed_fixed.astype(jnp.float32) * bed_unit).reshape(1, 1, 1, rows_x, rows_y)
    levels = jnp.arange(friction_table.shape[0], dtype=jnp.int32)
    chosen = (friction_rows[:, None] == levels[None, :]).astype(jnp.float32)
    friction = jnp.sum(chosen[:, :, None, None] * friction_table[None], axis=1)
    bottom = (
        (jnp.arange(layers, dtype=jnp.int32) == 0).astype(jnp.float32).reshape(1, 1, layers, 1, 1)
    )
    mask_block = cover.reshape(1, 1, 1, rows_x, rows_y)
    friction_block = friction.reshape(members, 1, 1, rows_x, rows_y)
    prior_wide, bed_wide, mask_wide, friction_wide = (
        extended_2(u_prior, (("plane", 3), ("planey", 4)), 4),
        extended_2(bed_block, (("plane", 3), ("planey", 4)), 4),
        extended_2(mask_block, (("plane", 3), ("planey", 4)), 4),
        extended_2(friction_block, (("plane", 3), ("planey", 4)), 4),
    )
    roots_three = trimmed(mask_wide, 1) * strain_roots(prior_wide)
    across_two = neighbour_sum(pad_layers(roots_three))
    bed_three = trimmed(bed_wide, 1)
    slope_x = (bed_three[..., 2:, 1:-1] - bed_three[..., :-2, 1:-1]) * 0.5
    slope_y = (bed_three[..., 1:-1, 2:] - bed_three[..., 1:-1, :-2]) * 0.5
    mask_two = trimmed(mask_wide, 2)
    position = (
        lax.axis_index("plane") * rows_x - 2 + jnp.arange(rows_x + 4, dtype=jnp.int32)
    ).astype(jnp.float32)
    thickness = 1.0 + 2.0 * position[:, None] / (total_x - 1)
    force_two = jnp.concatenate(
        [-(mask_two * thickness * slope_x), -(mask_two * thickness * slope_y)], axis=1
    )
    diag_two = mask_two * trimmed(friction_wide, 2) * bottom + (1.0 - mask_two)
    start_three = trimmed(prior_wide, 1) * trimmed(mask_wide, 1)
    residual_two = force_two - apply_local(roots_three, across_two, diag_two, start_three)
    image_one = apply_local(
        trimmed(roots_three, 1), trimmed(across_two, 1), trimmed(diag_two, 1), residual_two
    )
    second_image = apply_local(
        trimmed(roots_three, 2), trimmed(across_two, 2), trimmed(diag_two, 2), image_one
    )
    residual = trimmed(residual_two, 2)
    image = trimmed(image_one, 1)
    gram_rr, gram_ra, gram_aa, gram_ab = lax.psum(
        (
            inner(residual, residual),
            inner(residual, image),
            inner(image, image),
            inner(image, second_image),
        ),
        ("plane", "planey"),
    )
    first_step = gram_rr / gram_ra
    norm_next = gram_rr - 2.0 * first_step * gram_ra + first_step * first_step * gram_aa
    growth = 1.0 + norm_next / gram_rr
    curve = (
        growth * growth * gram_ra
        - 2.0 * growth * first_step * gram_aa
        + first_step * first_step * gram_ab
    )
    second_step = norm_next / curve
    solution = trimmed(start_three, 3)
    solution = (
        solution
        + spread(first_step + second_step * growth) * residual
        - spread(second_step * first_step) * image
    )
    local_sum = jnp.sum(solution, axis=0)
    summed = lax.psum(local_sum, "ens")
    return summed / (members * lax.axis_size("ens"))


def solution(mesh):
    in_specs = (
        P(("group", "ens"), None, None, "plane", "planey"),
        P(("group", "ens")),
        P("group", "plane", "planey"),
        P("plane", "planey"),
        P("plane", "planey"),
    )
    out_specs = P("group", None, "plane", "planey")
    return jax.shard_map(body, mesh=mesh, in_specs=in_specs, out_specs=out_specs, check_vma=False)
```

profile of v0, /device:TPU:0, one launch (start us, length us, event | category | flops | bytes accessed | tf_op | source)
XLA Modules:
  0.0 144.7 jit_solution(11222235841737665456)
XLA Ops:
  6.5 0.7 convert_bitcast_fusion
  7.2 4.9 %collective-permute-start.4 = (f32[1,1,1,4,128]{4,3,2,1,0:T(4,128)S(1)}, f32[1,1,1,4,128]{4,3,2,1,0:T(4,128)S(1)}, u32[]{:S(2)}, u32[]{:S(2)}) collective-permute-start(f32[1,1,1,4,128]{4,3,2,1,0:T(4,128)S(1)} %get-tuple-element.72), channel_id=1, source_target_pairs={{0,4},{4,8},{8,12},{1,5},{5,9},{9,13},{2,6},{6,10},{10,14},{3,7},{... | collective-permute-start | bytes 6152 | tf_op jit(solution)/shard_map/ppermute | solution.py:19
  12.2 1.3 collective-permute-start.5
  13.5 0.7 multiply_bitcast_fusion
  14.2 4.5 %collective-permute-start.8 = (f32[1,1,1,4,128]{4,3,2,1,0:T(4,128)S(1)}, f32[1,1,1,4,128]{4,3,2,1,0:T(4,128)S(1)}, u32[]{:S(2)}, u32[]{:S(2)}) collective-permute-start(f32[1,1,1,4,128]{4,3,2,1,0:T(4,128)S(1)} %get-tuple-element.70), channel_id=1, source_target_pairs={{0,4},{4,8},{8,12},{1,5},{5,9},{9,13},{2,6},{6,10},{10,14},{3,7},{... | collective-permute-start | bytes 6152 | tf_op jit(solution)/shard_map/ppermute | solution.py:19
  18.7 1.3 collective-permute-start.9
  20.0 0.7 compare_convert_fusion.1
  20.8 1.0 multiply_reduce_fusion.3
  21.8 4.5 %collective-permute-start.12 = (f32[2,1,1,4,128]{4,3,0,2,1:T(4,128)S(1)}, f32[2,1,1,4,128]{4,3,0,2,1:T(4,128)S(1)}, u32[]{:S(2)}, u32[]{:S(2)}) collective-permute-start(f32[2,1,1,4,128]{4,3,0,2,1:T(4,128)S(1)} %get-tuple-element.64), channel_id=1, source_target_pairs={{0,4},{4,8},{8,12},{1,5},{5,9},{9,13},{2,6},{6,10},{10,14},{3,7},{... | collective-permute-start | bytes 12296 | tf_op jit(solution)/shard_map/ppermute | solution.py:19
  26.4 1.0 fusion.197
  27.4 1.3 collective-permute-start.13
  28.7 4.6 %collective-permute-start = (f32[2,2,10,4,128]{4,3,2,1,0:T(4,128)S(1)}, f32[2,2,10,4,128]{4,3,2,1,0:T(4,128)S(1)}, u32[]{:S(2)}, u32[]{:S(2)}) collective-permute-start(f32[2,2,10,4,128]{4,3,2,1,0:T(4,128)S(1)} %get-tuple-element.56), channel_id=1, source_target_pairs={{0,4},{4,8},{8,12},{1,5},{5,9},{9,13},{2,6},{6,10},{10,14},{3,7},{... | collective-permute-start | bytes 245768 | tf_op jit(solution)/shard_map/ppermute | solution.py:19
  33.3 0.1 fusion.201
  33.4 3.4 %collective-permute-start.6 = (f32[1,1,1,24,4]{4,3,2,1,0:T(8,128)S(1)}, f32[1,1,1,24,4]{4,3,2,1,0:T(8,128)S(1)}, u32[]{:S(2)}, u32[]{:S(2)}) collective-permute-start(f32[1,1,1,24,4]{4,3,2,1,0:T(8,128)S(1)} %get-tuple-element.68), channel_id=1, source_target_pairs={{0,2},{1,3},{4,6},{5,7},{8,10},{9,11},{12,14},{13,15},{16,18},{17,... | collective-permute-start | bytes 1160 | tf_op jit(solution)/shard_map/ppermute | solution.py:19
  36.8 1.3 collective-permute-start.7
  38.1 0.1 fusion.200
  38.2 4.5 %collective-permute-start.10 = (f32[1,1,1,24,4]{4,3,2,1,0:T(8,128)S(1)}, f32[1,1,1,24,4]{4,3,2,1,0:T(8,128)S(1)}, u32[]{:S(2)}, u32[]{:S(2)}) collective-permute-start(f32[1,1,1,24,4]{4,3,2,1,0:T(8,128)S(1)} %get-tuple-element.66), channel_id=1, source_target_pairs={{0,2},{1,3},{4,6},{5,7},{8,10},{9,11},{12,14},{13,15},{16,18},{17,... | collective-permute-start | bytes 1160 | tf_op jit(solution)/shard_map/ppermute | solution.py:19
  42.7 1.3 collective-permute-start.11
  44.0 0.1 pad_maximum_fusion.6
  44.1 0.0 collective-permute-done.10
  44.1 1.3 collective-permute-start.1
  45.4 2.9 %collective-permute-done.11 = f32[1,1,1,24,4]{4,3,2,1,0:T(8,128)S(1)} collective-permute-done((f32[1,1,1,24,4]{4,3,2,1,0:T(8,128)S(1)}, f32[1,1,1,24,4]{4,3,2,1,0:T(8,128)S(1)}, u32[]{:S(2)}, u32[]{:S(2)}) %collective-permute-start.11) | collective-permute-done | bytes 416 | tf_op jit(solution)/shard_map/ppermute | solution.py:21
  48.3 0.1 pad_maximum_fusion.7
  48.4 0.1 fusion.193
  48.5 0.1 slice_bitcast_fusion.9
  48.6 0.1 fusion.198
  48.7 1.6 %collective-permute-start.14 = (f32[2,1,1,24,4]{4,3,0,2,1:T(8,128)S(1)}, f32[2,1,1,24,4]{4,3,0,2,1:T(8,128)S(1)}, u32[]{:S(2)}, u32[]{:S(2)}) collective-permute-start(f32[2,1,1,24,4]{4,3,0,2,1:T(8,128)S(1)} %get-tuple-element.62), channel_id=1, source_target_pairs={{0,2},{1,3},{4,6},{5,7},{8,10},{9,11},{12,14},{13,15},{16,18},{17,... | collective-permute-start | bytes 2312 | tf_op jit(solution)/shard_map/ppermute | solution.py:19
  50.4 1.3 collective-permute-start.15
  51.7 0.2 collective-permute-done.14
  51.9 4.2 %collective-permute-done.15 = f32[2,1,1,24,4]{4,3,0,2,1:T(8,128)S(1)} collective-permute-done((f32[2,1,1,24,4]{4,3,0,2,1:T(8,128)S(1)}, f32[2,1,1,24,4]{4,3,0,2,1:T(8,128)S(1)}, u32[]{:S(2)}, u32[]{:S(2)}) %collective-permute-start.15) | collective-permute-done | bytes 800 | tf_op jit(solution)/shard_map/ppermute | solution.py:21
  56.1 0.1 fusion.187
  56.2 0.0 copy-start
  56.2 0.1 multiply_add_fusion
  56.3 0.2 slice_bitcast_fusion
  56.5 0.1 multiply_add_fusion.1
  56.7 0.5 copy-done
  57.2 0.1 pad_maximum_fusion.1
  57.2 0.2 fusion.196
  57.4 1.7 %collective-permute-start.2 = (f32[2,2,10,24,4]{4,3,2,1,0:T(8,128)S(1)}, f32[2,2,10,24,4]{4,3,2,1,0:T(8,128)S(1)}, u32[]{:S(2)}, u32[]{:S(2)}) collective-permute-start(f32[2,2,10,24,4]{4,3,2,1,0:T(8,128)S(1)} %get-tuple-element.54), channel_id=1, source_target_pairs={{0,2},{1,3},{4,6},{5,7},{8,10},{9,11},{12,14},{13,15},{16,18},{17,... | collective-permute-start | bytes 46088 | tf_op jit(solution)/shard_map/ppermute | solution.py:19
  59.1 1.3 collective-permute-start.3
  60.4 0.1 slice_bitcast_fusion.7
  60.5 4.9 %collective-permute-done.2 = f32[2,2,10,24,4]{4,3,2,1,0:T(8,128)S(1)} collective-permute-done((f32[2,2,10,24,4]{4,3,2,1,0:T(8,128)S(1)}, f32[2,2,10,24,4]{4,3,2,1,0:T(8,128)S(1)}, u32[]{:S(2)}, u32[]{:S(2)}) %collective-permute-start.2) | collective-permute-done | bytes 15392 | tf_op jit(solution)/shard_map/ppermute | solution.py:19
  65.4 4.4 %collective-permute-done.3 = f32[2,2,10,24,4]{4,3,2,1,0:T(8,128)S(1)} collective-permute-done((f32[2,2,10,24,4]{4,3,2,1,0:T(8,128)S(1)}, f32[2,2,10,24,4]{4,3,2,1,0:T(8,128)S(1)}, u32[]{:S(2)}, u32[]{:S(2)}) %collective-permute-start.3) | collective-permute-done | bytes 15392 | tf_op jit(solution)/shard_map/ppermute | solution.py:21
  69.8 0.6 pad_maximum_fusion
  70.5 1.3 fusion.95
  71.8 0.5 fusion.101
  72.3 5.0 %fusion.103 = (f32[2,10,20,132]{3,2,1,0:T(8,128)S(1)}, f32[2,10,20,132]{3,2,1,0:T(8,128)}, f32[2,10,20,132]{3,2,1,0:T(8,128)}, f32[2,10,20,132]{3,2,1,0:T(8,128)...) fusion(f32[2,1,10,22,134]{4,3,2,1,0:T(8,128)S(1)} %fusion.101), kind=kLoop, calls=%fused_computation.200 | loop fusion | flops 580800 | bytes 4995840 | tf_op jit(solution)/shard_map/mul | solution.py:55
  77.3 2.6 %fusion.133 = (f32[2,10,20,132]{3,2,1,0:T(8,128)}, f32[2,10,20,132]{3,2,1,0:T(8,128)}, f32[2,10,20,132]{3,2,1,0:T(8,128)}, f32[2,10,20,132]{3,2,1,0:T(8,128)}, f...) fusion(f32[2,1,10,22,134]{4,3,2,1,0:T(8,128)S(1)} %fusion.101), kind=kLoop, calls=%fused_computation.240 | loop fusion | flops 158400 | bytes 3379200 | tf_op jit(solution)/shard_map/mul | solution.py:55
  79.9 1.0 slice_bitcast_fusion.1
  80.9 0.8 slice_bitcast_fusion.8
  81.7 0.3 broadcast_multiply_fusion.1
  82.0 0.3 copy-done.2
  82.3 0.0 copy-done.3
  82.3 0.0 copy-done.4
  82.4 0.0 copy-done.5
  82.4 8.9 %broadcast_multiply_fusion.2 = (f32[2,2,10,20,132]{4,3,2,1,0:T(8,128)S(1)}, f32[2,2,10,20,132]{4,3,2,1,0:T(8,128)S(1)}, f32[2,2,10,20,132]{4,3,2,1,0:T(8,128)S(1)}) fusion(f32[2,10,20,132]{3,2,1,0:T(8,128)} %get-tuple-element.53, f32[2,10,20,132]{3,2,1,0:T(8,128)S(1)} %multiply_add_fusion.1, f32[2,2,10,22,134]{4,3,2,1,0:T(8,128)S(1)} %get-tuple-element.21, ...), kind=kLoop, calls=%fused_computation.252 | loop fusion | flops 10032000 | bytes 17623040 | tf_op jit(solution)/shard_map/mul | solution.py:99
  91.3 0.0 copy-start.1
  91.3 5.9 %broadcast_multiply_fusion = (f32[2,2,10,18,130]{4,3,2,1,0:T(8,128)S(1)}, f32[2,2,10,18,130]{4,3,2,1,0:T(8,128)S(1)}) fusion(f32[2,10,18,130]{3,2,1,0:T(8,128)} %slice_bitcast_fusion.1, f32[2,10,18,130]{3,2,1,0:T(8,128)S(1)} %slice_bitcast_fusion, f32[2,2,10,20,132]{4,3,2,1,0:T(8,128)S(1)} %get-tuple-element.18, f32[2]{0:T(128)S(1)} %copy-done.5, ...), kind=kLoop, calls=%fused_computation.249 | loop fusion | flops 5335200 | bytes 12243008 | tf_op jit(solution)/shard_map/mul | solution.py:99
  97.2 1.8 %multiply_reduce_fusion.1 = (f32[2]{0:T(128)S(1)}, f32[2]{0:T(128)S(1)}, f32[2]{0:T(128)S(1)}, f32[2]{0:T(128)S(1)}) fusion(f32[2,2,10,20,132]{4,3,2,1,0:T(8,128)S(1)} %get-tuple-element.19, f32[2,2,10,18,130]{4,3,2,1,0:T(8,128)S(1)} %get-tuple-element.17, f32[2,10,16,128]{3,2,1,0:T(8,128)S(1)} %slice_bitcast_fusion.7, ...), kind=kLoop, calls=%fused_computation.313 | loop fusion | flops 5242872 | bytes 4917280 | tf_op jit(solution)/shard_map/reduce_sum | solution.py:87
  99.0 20.8 %all-reduce.5 = (f32[2]{0:T(128)S(1)}, f32[2]{0:T(128)S(1)}, f32[2]{0:T(128)S(1)}, f32[2]{0:T(128)S(1)}) all-reduce(f32[2]{0:T(128)S(1)} %get-tuple-element.23, f32[2]{0:T(128)S(1)} %get-tuple-element.6, f32[2]{0:T(128)S(1)} %get-tuple-element.7, ...), channel_id=1, replica_groups=mesh['group'=2,'plane'=4,'planey'=2,'ens'=2] {'plane','planey'}, use_global_device_ids=true, to_apply=%region_8.9 | all-reduce | flops 8 | bytes 64 | tf_op jit(solution)/shard_map/psum | solution.py:151
  119.8 1.0 fusion.184
  120.8 0.0 all-reduce.8.cloned.1.call-update
  120.8 15.4 %all-reduce.8.cloned.1.call-done = f32[2,10,16,128]{3,2,1,0:T(8,128)} async-done(((f32[2,10,16,128]{3,2,1,0:T(8,128)}), f32[2,10,16,128]{3,2,1,0:T(8,128)}) %all-reduce.8.cloned.1.call-update) | async-done | bytes 163856 | tf_op jit(solution)/shard_map/psum | solution.py:176
  136.3 1.6 %broadcast_multiply_fusion.3 = f32[2,10,16,128]{3,2,1,0:T(8,128)} fusion(f32[2,10,16,128]{3,2,1,0:T(8,128)} %all-reduce.8.cloned.1.call-done), kind=kLoop, calls=%fused_computation.319 | loop fusion | flops 40960 | bytes 327680 | tf_op jit(solution)/shard_map/div | solution.py:177
  (28 shorter events, 0.1 us)
Async XLA Ops:
  6.5 129.7 %all-reduce.8.cloned.1.call-start = ((), (), s32[]{:S(2)}) async-start(), calls=%async_computation | async-start | bytes 327680 | tf_op jit(solution)/shard_map/psum | solution.py:176
  7.2 20.2 %collective-permute-start.4 = (f32[1,1,1,4,128]{4,3,2,1,0:T(4,128)S(1)}, f32[1,1,1,4,128]{4,3,2,1,0:T(4,128)S(1)}, u32[]{:S(2)}, u32[]{:S(2)}) collective-permute-start(f32[1,1,1,4,128]{4,3,2,1,0:T(4,128)S(1)} %get-tuple-element.72), channel_id=1, source_target_pairs={{0,4},{4,8},{8,12},{1,5},{5,9},{9,13},{2,6},{6,10},{10,14},{3,7},{... | collective-permute-start | bytes 6152 | tf_op jit(solution)/shard_map/ppermute | solution.py:19
  12.2 16.5 %collective-permute-start.5 = (f32[1,1,1,4,128]{4,3,2,1,0:T(4,128)S(1)}, f32[1,1,1,4,128]{4,3,2,1,0:T(4,128)S(1)}, u32[]{:S(2)}, u32[]{:S(2)}) collective-permute-start(f32[1,1,1,4,128]{4,3,2,1,0:T(4,128)S(1)} %get-tuple-element.73), channel_id=1, source_target_pairs={{4,0},{8,4},{12,8},{5,1},{9,5},{13,9},{6,2},{10,6},{14,10},{7,3},{... | collective-permute-start | bytes 6152 | tf_op jit(solution)/shard_map/ppermute | solution.py:21
  14.2 19.2 %collective-permute-start.8 = (f32[1,1,1,4,128]{4,3,2,1,0:T(4,128)S(1)}, f32[1,1,1,4,128]{4,3,2,1,0:T(4,128)S(1)}, u32[]{:S(2)}, u32[]{:S(2)}) collective-permute-start(f32[1,1,1,4,128]{4,3,2,1,0:T(4,128)S(1)} %get-tuple-element.70), channel_id=1, source_target_pairs={{0,4},{4,8},{8,12},{1,5},{5,9},{9,13},{2,6},{6,10},{10,14},{3,7},{... | collective-permute-start | bytes 6152 | tf_op jit(solution)/shard_map/ppermute | solution.py:19
  18.7 18.0 %collective-permute-start.9 = (f32[1,1,1,4,128]{4,3,2,1,0:T(4,128)S(1)}, f32[1,1,1,4,128]{4,3,2,1,0:T(4,128)S(1)}, u32[]{:S(2)}, u32[]{:S(2)}) collective-permute-start(f32[1,1,1,4,128]{4,3,2,1,0:T(4,128)S(1)} %get-tuple-element.71), channel_id=1, source_target_pairs={{4,0},{8,4},{12,8},{5,1},{9,5},{13,9},{6,2},{10,6},{14,10},{7,3},{... | collective-permute-start | bytes 6152 | tf_op jit(solution)/shard_map/ppermute | solution.py:21
  21.8 26.8 %collective-permute-start.12 = (f32[2,1,1,4,128]{4,3,0,2,1:T(4,128)S(1)}, f32[2,1,1,4,128]{4,3,0,2,1:T(4,128)S(1)}, u32[]{:S(2)}, u32[]{:S(2)}) collective-permute-start(f32[2,1,1,4,128]{4,3,0,2,1:T(4,128)S(1)} %get-tuple-element.64), channel_id=1, source_target_pairs={{0,4},{4,8},{8,12},{1,5},{5,9},{9,13},{2,6},{6,10},{10,14},{3,7},{... | collective-permute-start | bytes 12296 | tf_op jit(solution)/shard_map/ppermute | solution.py:19
  27.4 21.2 %collective-permute-start.13 = (f32[2,1,1,4,128]{4,3,0,2,1:T(4,128)S(1)}, f32[2,1,1,4,128]{4,3,0,2,1:T(4,128)S(1)}, u32[]{:S(2)}, u32[]{:S(2)}) collective-permute-start(f32[2,1,1,4,128]{4,3,0,2,1:T(4,128)S(1)} %get-tuple-element.65), channel_id=1, source_target_pairs={{4,0},{8,4},{12,8},{5,1},{9,5},{13,9},{6,2},{10,6},{14,10},{7,3},{... | collective-permute-start | bytes 12296 | tf_op jit(solution)/shard_map/ppermute | solution.py:21
  28.7 27.9 %collective-permute-start = (f32[2,2,10,4,128]{4,3,2,1,0:T(4,128)S(1)}, f32[2,2,10,4,128]{4,3,2,1,0:T(4,128)S(1)}, u32[]{:S(2)}, u32[]{:S(2)}) collective-permute-start(f32[2,2,10,4,128]{4,3,2,1,0:T(4,128)S(1)} %get-tuple-element.56), channel_id=1, source_target_pairs={{0,4},{4,8},{8,12},{1,5},{5,9},{9,13},{2,6},{6,10},{10,14},{3,7},{... | collective-permute-start | bytes 245768 | tf_op jit(solution)/shard_map/ppermute | solution.py:19
  33.4 4.8 %collective-permute-start.6 = (f32[1,1,1,24,4]{4,3,2,1,0:T(8,128)S(1)}, f32[1,1,1,24,4]{4,3,2,1,0:T(8,128)S(1)}, u32[]{:S(2)}, u32[]{:S(2)}) collective-permute-start(f32[1,1,1,24,4]{4,3,2,1,0:T(8,128)S(1)} %get-tuple-element.68), channel_id=1, source_target_pairs={{0,2},{1,3},{4,6},{5,7},{8,10},{9,11},{12,14},{13,15},{16,18},{17,... | collective-permute-start | bytes 1160 | tf_op jit(solution)/shard_map/ppermute | solution.py:19
  36.8 5.9 %collective-permute-start.7 = (f32[1,1,1,24,4]{4,3,2,1,0:T(8,128)S(1)}, f32[1,1,1,24,4]{4,3,2,1,0:T(8,128)S(1)}, u32[]{:S(2)}, u32[]{:S(2)}) collective-permute-start(f32[1,1,1,24,4]{4,3,2,1,0:T(8,128)S(1)} %get-tuple-element.69), channel_id=1, source_target_pairs={{2,0},{3,1},{6,4},{7,5},{10,8},{11,9},{14,12},{15,13},{18,16},{19,... | collective-permute-start | bytes 1160 | tf_op jit(solution)/shard_map/ppermute | solution.py:21
  38.2 5.9 %collective-permute-start.10 = (f32[1,1,1,24,4]{4,3,2,1,0:T(8,128)S(1)}, f32[1,1,1,24,4]{4,3,2,1,0:T(8,128)S(1)}, u32[]{:S(2)}, u32[]{:S(2)}) collective-permute-start(f32[1,1,1,24,4]{4,3,2,1,0:T(8,128)S(1)} %get-tuple-element.66), channel_id=1, source_target_pairs={{0,2},{1,3},{4,6},{5,7},{8,10},{9,11},{12,14},{13,15},{16,18},{17,... | collective-permute-start | bytes 1160 | tf_op jit(solution)/shard_map/ppermute | solution.py:19
  42.7 5.6 %collective-permute-start.11 = (f32[1,1,1,24,4]{4,3,2,1,0:T(8,128)S(1)}, f32[1,1,1,24,4]{4,3,2,1,0:T(8,128)S(1)}, u32[]{:S(2)}, u32[]{:S(2)}) collective-permute-start(f32[1,1,1,24,4]{4,3,2,1,0:T(8,128)S(1)} %get-tuple-element.67), channel_id=1, source_target_pairs={{2,0},{3,1},{6,4},{7,5},{10,8},{11,9},{14,12},{15,13},{18,16},{19,... | collective-permute-start | bytes 1160 | tf_op jit(solution)/shard_map/ppermute | solution.py:21
  44.1 12.5 %collective-permute-start.1 = (f32[2,2,10,4,128]{4,3,2,1,0:T(4,128)S(1)}, f32[2,2,10,4,128]{4,3,2,1,0:T(4,128)S(1)}, u32[]{:S(2)}, u32[]{:S(2)}) collective-permute-start(f32[2,2,10,4,128]{4,3,2,1,0:T(4,128)S(1)} %get-tuple-element.57), channel_id=1, source_target_pairs={{4,0},{8,4},{12,8},{5,1},{9,5},{13,9},{6,2},{10,6},{14,10},{7,3},{... | collective-permute-start | bytes 245768 | tf_op jit(solution)/shard_map/ppermute | solution.py:21
  48.7 3.2 %collective-permute-start.14 = (f32[2,1,1,24,4]{4,3,0,2,1:T(8,128)S(1)}, f32[2,1,1,24,4]{4,3,0,2,1:T(8,128)S(1)}, u32[]{:S(2)}, u32[]{:S(2)}) collective-permute-start(f32[2,1,1,24,4]{4,3,0,2,1:T(8,128)S(1)} %get-tuple-element.62), channel_id=1, source_target_pairs={{0,2},{1,3},{4,6},{5,7},{8,10},{9,11},{12,14},{13,15},{16,18},{17,... | collective-permute-start | bytes 2312 | tf_op jit(solution)/shard_map/ppermute | solution.py:19
  50.4 5.7 %collective-permute-start.15 = (f32[2,1,1,24,4]{4,3,0,2,1:T(8,128)S(1)}, f32[2,1,1,24,4]{4,3,0,2,1:T(8,128)S(1)}, u32[]{:S(2)}, u32[]{:S(2)}) collective-permute-start(f32[2,1,1,24,4]{4,3,0,2,1:T(8,128)S(1)} %get-tuple-element.63), channel_id=1, source_target_pairs={{2,0},{3,1},{6,4},{7,5},{10,8},{11,9},{14,12},{15,13},{18,16},{19,... | collective-permute-start | bytes 2312 | tf_op jit(solution)/shard_map/ppermute | solution.py:21
  56.2 1.0 copy-start
  57.4 8.0 %collective-permute-start.2 = (f32[2,2,10,24,4]{4,3,2,1,0:T(8,128)S(1)}, f32[2,2,10,24,4]{4,3,2,1,0:T(8,128)S(1)}, u32[]{:S(2)}, u32[]{:S(2)}) collective-permute-start(f32[2,2,10,24,4]{4,3,2,1,0:T(8,128)S(1)} %get-tuple-element.54), channel_id=1, source_target_pairs={{0,2},{1,3},{4,6},{5,7},{8,10},{9,11},{12,14},{13,15},{16,18},{17,... | collective-permute-start | bytes 46088 | tf_op jit(solution)/shard_map/ppermute | solution.py:19
  59.1 10.7 %collective-permute-start.3 = (f32[2,2,10,24,4]{4,3,2,1,0:T(8,128)S(1)}, f32[2,2,10,24,4]{4,3,2,1,0:T(8,128)S(1)}, u32[]{:S(2)}, u32[]{:S(2)}) collective-permute-start(f32[2,2,10,24,4]{4,3,2,1,0:T(8,128)S(1)} %get-tuple-element.55), channel_id=1, source_target_pairs={{2,0},{3,1},{6,4},{7,5},{10,8},{11,9},{14,12},{15,13},{18,16},{19,... | collective-permute-start | bytes 46088 | tf_op jit(solution)/shard_map/ppermute | solution.py:21
  81.7 0.7 copy-start.2
  81.7 0.7 copy-start.3
  81.7 0.7 copy-start.4
  81.7 0.7 copy-start.5
  91.3 5.9 %copy-start.1 = (f32[2,10,16,128]{3,2,1,0:T(8,128)S(1)}, f32[2,10,16,128]{3,2,1,0:T(8,128)}, u32[]{:S(2)}) copy-start(f32[2,10,16,128]{3,2,1,0:T(8,128)} %slice_bitcast_fusion.8) | copy-start | bytes 491524
Sparse Core Ops, SparseCore 0:
  120.9 15.2 all-reduce.7
where the time goes:
time: 146 us; the launch traced here: 145 us
  starting transfers between devices  40.1 us (27%)
  other arithmetic  33.4 us (23%)
  waiting for transfers between devices  32.1 us (22%)
  blocking collectives  20.8 us (14%)
  between operations  13.8 us (9%)
  local copies, waits for them, and re-layouts  4.52 us (3%)
    ppermute x8, starting transfers between devices, extended_2(): lax.ppermute(tail, axis, [(i, (i + 1) % count) for i in range(ends)])  29.8 us
    psum x1, blocking collectives, body(): lax.psum((inner(residual, residual), inner(residual, image), inner(image,...  20.8 us
    psum x1, waiting for transfers between devices, body(): summed = lax.psum(local_sum, 'ens')  15.4 us
    mul x3, other arithmetic, apply_local(): product = roots_wide * field_wide  15.1 us
    ppermute x8, waiting for transfers between devices, extended_2(): lax.ppermute(head, axis, [((i + 1) % count, i) for i in range(ends)])  11.6 us
    ppermute x8, starting transfers between devices, extended_2(): lax.ppermute(head, axis, [((i + 1) % count, i) for i in range(ends)])  10.3 us
    mul x2, other arithmetic, neighbour_sum(): addend = coefficient((step_z, step_x, step_y)) * window  7.6 us
    ppermute x8, waiting for transfers between devices, extended_2(): lax.ppermute(tail, axis, [(i, (i + 1) % count) for i in range(ends)])  5.09 us
  transfers between devices with their start and end apart: 17, of which 6 were waited for; matrix products, arithmetic and copies ran while one was open for 3% of the time, Pallas kernels for 0%

commit v1 on v0

--- a/solution.py
+++ b/solution.py
@@ -173,7 +173,7 @@
         - spread(second_step * first_step) * image
     )
     local_sum = jnp.sum(solution, axis=0)
-    summed = lax.psum(local_sum, "ens")
+    summed = jnp.sum(lax.all_gather(local_sum, "ens"), axis=0)
     return summed / (members * lax.axis_size("ens"))
 
 

time: 146 us -> 117 us (0.80)
  waiting for transfers between devices: 32.1 us -> 16.6 us
  between operations: 13.8 us -> 0.4 us
  blocking collectives: 20.8 us -> 22.8 us
  other arithmetic: 33.4 us -> 31.8 us
    psum x1 -> x0, waiting for transfers between devices: 15.4 us -> none  [body(): summed = lax.psum(local_sum, 'ens')]
    all_gather x0 -> x1, blocking collectives: none -> 2.04 us  [body(): summed = jnp.sum(lax.all_gather(local_sum, 'ens'), axis=0)]
  transfers between devices with their start and end apart: 17 -> 16, of which waited for: 6 -> 5; matrix products, arithmetic and copies ran while one was open for 3% -> 4% of each run, Pallas kernels for 0% -> 0%
where the time goes in v1:
time: 117 us; the launch traced here: 116 us
  starting transfers between devices  40.1 us (34%)
  other arithmetic  31.8 us (27%)
  blocking collectives  22.8 us (19%)
  waiting for transfers between devices  16.6 us (14%)
  local copies, waits for them, and re-layouts  4.52 us (4%)
    ppermute x8, starting transfers between devices, extended_2(): lax.ppermute(tail, axis, [(i, (i + 1) % count) for i in range(ends)])  29.8 us
    psum x1, blocking collectives, body(): lax.psum((inner(residual, residual), inner(residual, image), inner(image,...  20.8 us
    mul x3, other arithmetic, apply_local(): product = roots_wide * field_wide  15.1 us
    ppermute x8, waiting for transfers between devices, extended_2(): lax.ppermute(head, axis, [((i + 1) % count, i) for i in range(ends)])  11.6 us
    ppermute x8, starting transfers between devices, extended_2(): lax.ppermute(head, axis, [((i + 1) % count, i) for i in range(ends)])  10.3 us
    mul x2, other arithmetic, neighbour_sum(): addend = coefficient((step_z, step_x, step_y)) * window  7.59 us
    ppermute x8, waiting for transfers between devices, extended_2(): lax.ppermute(tail, axis, [(i, (i + 1) % count) for i in range(ends)])  5.09 us
  transfers between devices with their start and end apart: 16, of which 5 were waited for; matrix products, arithmetic and copies ran while one was open for 4% of the time, Pallas kernels for 0%

profile of v1, /device:TPU:0, one launch (start us, length us, event | category | flops | bytes accessed | tf_op | source)
XLA Modules:
  0.0 116.3 jit_solution(5246089524926820661)
XLA Ops:
  0.0 0.7 convert_bitcast_fusion
  0.7 4.9 %collective-permute-start.4 = (f32[1,1,1,4,128]{4,3,2,1,0:T(4,128)S(1)}, f32[1,1,1,4,128]{4,3,2,1,0:T(4,128)S(1)}, u32[]{:S(2)}, u32[]{:S(2)}) collective-permute-start(f32[1,1,1,4,128]{4,3,2,1,0:T(4,128)S(1)} %get-tuple-element.72), channel_id=1, source_target_pairs={{0,4},{4,8},{8,12},{1,5},{5,9},{9,13},{2,6},{6,10},{10,14},{3,7},{... | collective-permute-start | bytes 6152 | tf_op jit(solution)/shard_map/ppermute | solution.py:19
  5.7 1.3 %collective-permute-start.5 = (f32[1,1,1,4,128]{4,3,2,1,0:T(4,128)S(1)}, f32[1,1,1,4,128]{4,3,2,1,0:T(4,128)S(1)}, u32[]{:S(2)}, u32[]{:S(2)}) collective-permute-start(f32[1,1,1,4,128]{4,3,2,1,0:T(4,128)S(1)} %get-tuple-element.73), channel_id=1, source_target_pairs={{4,0},{8,4},{12,8},{5,1},{9,5},{13,9},{6,2},{10,6},{14,10},{7,3},{... | collective-permute-start | bytes 6152 | tf_op jit(solution)/shard_map/ppermute | solution.py:21
  7.0 0.7 multiply_bitcast_fusion
  7.7 4.5 %collective-permute-start.8 = (f32[1,1,1,4,128]{4,3,2,1,0:T(4,128)S(1)}, f32[1,1,1,4,128]{4,3,2,1,0:T(4,128)S(1)}, u32[]{:S(2)}, u32[]{:S(2)}) collective-permute-start(f32[1,1,1,4,128]{4,3,2,1,0:T(4,128)S(1)} %get-tuple-element.70), channel_id=1, source_target_pairs={{0,4},{4,8},{8,12},{1,5},{5,9},{9,13},{2,6},{6,10},{10,14},{3,7},{... | collective-permute-start | bytes 6152 | tf_op jit(solution)/shard_map/ppermute | solution.py:19
  12.2 1.3 %collective-permute-start.9 = (f32[1,1,1,4,128]{4,3,2,1,0:T(4,128)S(1)}, f32[1,1,1,4,128]{4,3,2,1,0:T(4,128)S(1)}, u32[]{:S(2)}, u32[]{:S(2)}) collective-permute-start(f32[1,1,1,4,128]{4,3,2,1,0:T(4,128)S(1)} %get-tuple-element.71), channel_id=1, source_target_pairs={{4,0},{8,4},{12,8},{5,1},{9,5},{13,9},{6,2},{10,6},{14,10},{7,3},{... | collective-permute-start | bytes 6152 | tf_op jit(solution)/shard_map/ppermute | solution.py:21
  13.5 0.7 compare_convert_fusion.1
  14.2 1.0 multiply_reduce_fusion.3
  15.3 4.5 %collective-permute-start.12 = (f32[2,1,1,4,128]{4,3,0,2,1:T(4,128)S(1)}, f32[2,1,1,4,128]{4,3,0,2,1:T(4,128)S(1)}, u32[]{:S(2)}, u32[]{:S(2)}) collective-permute-start(f32[2,1,1,4,128]{4,3,0,2,1:T(4,128)S(1)} %get-tuple-element.64), channel_id=1, source_target_pairs={{0,4},{4,8},{8,12},{1,5},{5,9},{9,13},{2,6},{6,10},{10,14},{3,7},{... | collective-permute-start | bytes 12296 | tf_op jit(solution)/shard_map/ppermute | solution.py:19
  19.8 1.0 fusion.197
  20.9 1.3 %collective-permute-start.13 = (f32[2,1,1,4,128]{4,3,0,2,1:T(4,128)S(1)}, f32[2,1,1,4,128]{4,3,0,2,1:T(4,128)S(1)}, u32[]{:S(2)}, u32[]{:S(2)}) collective-permute-start(f32[2,1,1,4,128]{4,3,0,2,1:T(4,128)S(1)} %get-tuple-element.65), channel_id=1, source_target_pairs={{4,0},{8,4},{12,8},{5,1},{9,5},{13,9},{6,2},{10,6},{14,10},{7,3},{... | collective-permute-start | bytes 12296 | tf_op jit(solution)/shard_map/ppermute | solution.py:21
  22.2 0.0 collective-permute-done.5
  22.2 4.6 %collective-permute-start = (f32[2,2,10,4,128]{4,3,2,1,0:T(4,128)S(1)}, f32[2,2,10,4,128]{4,3,2,1,0:T(4,128)S(1)}, u32[]{:S(2)}, u32[]{:S(2)}) collective-permute-start(f32[2,2,10,4,128]{4,3,2,1,0:T(4,128)S(1)} %get-tuple-element.56), channel_id=1, source_target_pairs={{0,4},{4,8},{8,12},{1,5},{5,9},{9,13},{2,6},{6,10},{10,14},{3,7},{... | collective-permute-start | bytes 245768 | tf_op jit(solution)/shard_map/ppermute | solution.py:19
  26.8 0.1 fusion.201
  26.9 3.4 %collective-permute-start.6 = (f32[1,1,1,24,4]{4,3,2,1,0:T(8,128)S(1)}, f32[1,1,1,24,4]{4,3,2,1,0:T(8,128)S(1)}, u32[]{:S(2)}, u32[]{:S(2)}) collective-permute-start(f32[1,1,1,24,4]{4,3,2,1,0:T(8,128)S(1)} %get-tuple-element.68), channel_id=1, source_target_pairs={{0,2},{1,3},{4,6},{5,7},{8,10},{9,11},{12,14},{13,15},{16,18},{17,... | collective-permute-start | bytes 1160 | tf_op jit(solution)/shard_map/ppermute | solution.py:19
  30.3 1.3 %collective-permute-start.7 = (f32[1,1,1,24,4]{4,3,2,1,0:T(8,128)S(1)}, f32[1,1,1,24,4]{4,3,2,1,0:T(8,128)S(1)}, u32[]{:S(2)}, u32[]{:S(2)}) collective-permute-start(f32[1,1,1,24,4]{4,3,2,1,0:T(8,128)S(1)} %get-tuple-element.69), channel_id=1, source_target_pairs={{2,0},{3,1},{6,4},{7,5},{10,8},{11,9},{14,12},{15,13},{18,16},{19,... | collective-permute-start | bytes 1160 | tf_op jit(solution)/shard_map/ppermute | solution.py:21
  31.6 0.1 fusion.200
  31.7 4.5 %collective-permute-start.10 = (f32[1,1,1,24,4]{4,3,2,1,0:T(8,128)S(1)}, f32[1,1,1,24,4]{4,3,2,1,0:T(8,128)S(1)}, u32[]{:S(2)}, u32[]{:S(2)}) collective-permute-start(f32[1,1,1,24,4]{4,3,2,1,0:T(8,128)S(1)} %get-tuple-element.66), channel_id=1, source_target_pairs={{0,2},{1,3},{4,6},{5,7},{8,10},{9,11},{12,14},{13,15},{16,18},{17,... | collective-permute-start | bytes 1160 | tf_op jit(solution)/shard_map/ppermute | solution.py:19
  36.2 1.3 %collective-permute-start.11 = (f32[1,1,1,24,4]{4,3,2,1,0:T(8,128)S(1)}, f32[1,1,1,24,4]{4,3,2,1,0:T(8,128)S(1)}, u32[]{:S(2)}, u32[]{:S(2)}) collective-permute-start(f32[1,1,1,24,4]{4,3,2,1,0:T(8,128)S(1)} %get-tuple-element.67), channel_id=1, source_target_pairs={{2,0},{3,1},{6,4},{7,5},{10,8},{11,9},{14,12},{15,13},{18,16},{19,... | collective-permute-start | bytes 1160 | tf_op jit(solution)/shard_map/ppermute | solution.py:21
  37.5 0.1 pad_maximum_fusion.6
  37.6 0.0 collective-permute-done.10
  37.6 1.3 %collective-permute-start.1 = (f32[2,2,10,4,128]{4,3,2,1,0:T(4,128)S(1)}, f32[2,2,10,4,128]{4,3,2,1,0:T(4,128)S(1)}, u32[]{:S(2)}, u32[]{:S(2)}) collective-permute-start(f32[2,2,10,4,128]{4,3,2,1,0:T(4,128)S(1)} %get-tuple-element.57), channel_id=1, source_target_pairs={{4,0},{8,4},{12,8},{5,1},{9,5},{13,9},{6,2},{10,6},{14,10},{7,3},{... | collective-permute-start | bytes 245768 | tf_op jit(solution)/shard_map/ppermute | solution.py:21
  38.9 2.9 %collective-permute-done.11 = f32[1,1,1,24,4]{4,3,2,1,0:T(8,128)S(1)} collective-permute-done((f32[1,1,1,24,4]{4,3,2,1,0:T(8,128)S(1)}, f32[1,1,1,24,4]{4,3,2,1,0:T(8,128)S(1)}, u32[]{:S(2)}, u32[]{:S(2)}) %collective-permute-start.11) | collective-permute-done | bytes 416 | tf_op jit(solution)/shard_map/ppermute | solution.py:21
  41.8 0.1 pad_maximum_fusion.7
  41.9 0.1 fusion.193
  42.0 0.1 slice_bitcast_fusion.9
  42.1 0.1 fusion.198
  42.2 1.6 %collective-permute-start.14 = (f32[2,1,1,24,4]{4,3,0,2,1:T(8,128)S(1)}, f32[2,1,1,24,4]{4,3,0,2,1:T(8,128)S(1)}, u32[]{:S(2)}, u32[]{:S(2)}) collective-permute-start(f32[2,1,1,24,4]{4,3,0,2,1:T(8,128)S(1)} %get-tuple-element.62), channel_id=1, source_target_pairs={{0,2},{1,3},{4,6},{5,7},{8,10},{9,11},{12,14},{13,15},{16,18},{17,... | collective-permute-start | bytes 2312 | tf_op jit(solution)/shard_map/ppermute | solution.py:19
  43.8 1.3 %collective-permute-start.15 = (f32[2,1,1,24,4]{4,3,0,2,1:T(8,128)S(1)}, f32[2,1,1,24,4]{4,3,0,2,1:T(8,128)S(1)}, u32[]{:S(2)}, u32[]{:S(2)}) collective-permute-start(f32[2,1,1,24,4]{4,3,0,2,1:T(8,128)S(1)} %get-tuple-element.63), channel_id=1, source_target_pairs={{2,0},{3,1},{6,4},{7,5},{10,8},{11,9},{14,12},{15,13},{18,16},{19,... | collective-permute-start | bytes 2312 | tf_op jit(solution)/shard_map/ppermute | solution.py:21
  45.1 0.2 collective-permute-done.14
  45.3 4.2 %collective-permute-done.15 = f32[2,1,1,24,4]{4,3,0,2,1:T(8,128)S(1)} collective-permute-done((f32[2,1,1,24,4]{4,3,0,2,1:T(8,128)S(1)}, f32[2,1,1,24,4]{4,3,0,2,1:T(8,128)S(1)}, u32[]{:S(2)}, u32[]{:S(2)}) %collective-permute-start.15) | collective-permute-done | bytes 800 | tf_op jit(solution)/shard_map/ppermute | solution.py:21
  49.5 0.1 fusion.187
  49.7 0.0 copy-start
  49.7 0.1 multiply_add_fusion
  49.8 0.2 slice_bitcast_fusion
  50.0 0.1 multiply_add_fusion.1
  50.1 0.5 copy-done
  50.6 0.1 pad_maximum_fusion.1
  50.7 0.2 fusion.196
  50.9 1.7 %collective-permute-start.2 = (f32[2,2,10,24,4]{4,3,2,1,0:T(8,128)S(1)}, f32[2,2,10,24,4]{4,3,2,1,0:T(8,128)S(1)}, u32[]{:S(2)}, u32[]{:S(2)}) collective-permute-start(f32[2,2,10,24,4]{4,3,2,1,0:T(8,128)S(1)} %get-tuple-element.54), channel_id=1, source_target_pairs={{0,2},{1,3},{4,6},{5,7},{8,10},{9,11},{12,14},{13,15},{16,18},{17,... | collective-permute-start | bytes 46088 | tf_op jit(solution)/shard_map/ppermute | solution.py:19
  52.6 1.3 %collective-permute-start.3 = (f32[2,2,10,24,4]{4,3,2,1,0:T(8,128)S(1)}, f32[2,2,10,24,4]{4,3,2,1,0:T(8,128)S(1)}, u32[]{:S(2)}, u32[]{:S(2)}) collective-permute-start(f32[2,2,10,24,4]{4,3,2,1,0:T(8,128)S(1)} %get-tuple-element.55), channel_id=1, source_target_pairs={{2,0},{3,1},{6,4},{7,5},{10,8},{11,9},{14,12},{15,13},{18,16},{19,... | collective-permute-start | bytes 46088 | tf_op jit(solution)/shard_map/ppermute | solution.py:21
  53.9 0.1 slice_bitcast_fusion.7
  54.0 4.9 %collective-permute-done.2 = f32[2,2,10,24,4]{4,3,2,1,0:T(8,128)S(1)} collective-permute-done((f32[2,2,10,24,4]{4,3,2,1,0:T(8,128)S(1)}, f32[2,2,10,24,4]{4,3,2,1,0:T(8,128)S(1)}, u32[]{:S(2)}, u32[]{:S(2)}) %collective-permute-start.2) | collective-permute-done | bytes 15392 | tf_op jit(solution)/shard_map/ppermute | solution.py:19
  58.9 4.4 %collective-permute-done.3 = f32[2,2,10,24,4]{4,3,2,1,0:T(8,128)S(1)} collective-permute-done((f32[2,2,10,24,4]{4,3,2,1,0:T(8,128)S(1)}, f32[2,2,10,24,4]{4,3,2,1,0:T(8,128)S(1)}, u32[]{:S(2)}, u32[]{:S(2)}) %collective-permute-start.3) | collective-permute-done | bytes 15392 | tf_op jit(solution)/shard_map/ppermute | solution.py:21
  63.3 0.6 pad_maximum_fusion
  63.9 1.3 %fusion.95 = (f32[2,2,10,22,134]{4,3,2,1,0:T(8,128)S(1)}, f32[2,2,10,22,134]{4,3,2,1,0:T(8,128)S(1)}, f32[2,2,10,22,134]{4,3,2,1,0:T(8,128)S(1)}) fusion(f32[2,2,10,24,136]{4,3,2,1,0:T(8,128)S(1)} %pad_maximum_fusion), kind=kLoop, calls=%fused_computation.169 | loop fusion | flops 707520 | bytes 6330240 | tf_op jit(solution)/shard_map/mul | solution.py:63
  65.2 0.5 fusion.101
  65.7 5.0 %fusion.103 = (f32[2,10,20,132]{3,2,1,0:T(8,128)S(1)}, f32[2,10,20,132]{3,2,1,0:T(8,128)}, f32[2,10,20,132]{3,2,1,0:T(8,128)}, f32[2,10,20,132]{3,2,1,0:T(8,128)...) fusion(f32[2,1,10,22,134]{4,3,2,1,0:T(8,128)S(1)} %fusion.101), kind=kLoop, calls=%fused_computation.200 | loop fusion | flops 580800 | bytes 4995840 | tf_op jit(solution)/shard_map/mul | solution.py:55
  70.8 2.6 %fusion.133 = (f32[2,10,20,132]{3,2,1,0:T(8,128)}, f32[2,10,20,132]{3,2,1,0:T(8,128)}, f32[2,10,20,132]{3,2,1,0:T(8,128)}, f32[2,10,20,132]{3,2,1,0:T(8,128)}, f...) fusion(f32[2,1,10,22,134]{4,3,2,1,0:T(8,128)S(1)} %fusion.101), kind=kLoop, calls=%fused_computation.240 | loop fusion | flops 158400 | bytes 3379200 | tf_op jit(solution)/shard_map/mul | solution.py:55
  73.3 1.0 slice_bitcast_fusion.1
  74.4 0.8 slice_bitcast_fusion.8
  75.1 0.3 broadcast_multiply_fusion.1
  75.5 0.3 copy-done.2
  75.8 0.0 copy-done.3
  75.8 0.0 copy-done.4
  75.8 0.0 copy-done.5
  75.8 8.9 %broadcast_multiply_fusion.2 = (f32[2,2,10,20,132]{4,3,2,1,0:T(8,128)S(1)}, f32[2,2,10,20,132]{4,3,2,1,0:T(8,128)S(1)}, f32[2,2,10,20,132]{4,3,2,1,0:T(8,128)S(1)}) fusion(f32[2,10,20,132]{3,2,1,0:T(8,128)} %get-tuple-element.53, f32[2,10,20,132]{3,2,1,0:T(8,128)S(1)} %multiply_add_fusion.1, f32[2,2,10,22,134]{4,3,2,1,0:T(8,128)S(1)} %get-tuple-element.21, ...), kind=kLoop, calls=%fused_computation.252 | loop fusion | flops 10032000 | bytes 17623040 | tf_op jit(solution)/shard_map/mul | solution.py:99
  84.7 0.0 copy-start.1
  84.8 5.9 %broadcast_multiply_fusion = (f32[2,2,10,18,130]{4,3,2,1,0:T(8,128)S(1)}, f32[2,2,10,18,130]{4,3,2,1,0:T(8,128)S(1)}) fusion(f32[2,10,18,130]{3,2,1,0:T(8,128)} %slice_bitcast_fusion.1, f32[2,10,18,130]{3,2,1,0:T(8,128)S(1)} %slice_bitcast_fusion, f32[2,2,10,20,132]{4,3,2,1,0:T(8,128)S(1)} %get-tuple-element.18, f32[2]{0:T(128)S(1)} %copy-done.5, ...), kind=kLoop, calls=%fused_computation.249 | loop fusion | flops 5335200 | bytes 12243008 | tf_op jit(solution)/shard_map/mul | solution.py:99
  90.6 1.8 %multiply_reduce_fusion.1 = (f32[2]{0:T(128)S(1)}, f32[2]{0:T(128)S(1)}, f32[2]{0:T(128)S(1)}, f32[2]{0:T(128)S(1)}) fusion(f32[2,2,10,20,132]{4,3,2,1,0:T(8,128)S(1)} %get-tuple-element.19, f32[2,2,10,18,130]{4,3,2,1,0:T(8,128)S(1)} %get-tuple-element.17, f32[2,10,16,128]{3,2,1,0:T(8,128)S(1)} %slice_bitcast_fusion.7, ...), kind=kLoop, calls=%fused_computation.313 | loop fusion | flops 5242872 | bytes 4917280 | tf_op jit(solution)/shard_map/reduce_sum | solution.py:87
  92.4 20.8 %all-reduce.5 = (f32[2]{0:T(128)S(1)}, f32[2]{0:T(128)S(1)}, f32[2]{0:T(128)S(1)}, f32[2]{0:T(128)S(1)}) all-reduce(f32[2]{0:T(128)S(1)} %get-tuple-element.23, f32[2]{0:T(128)S(1)} %get-tuple-element.6, f32[2]{0:T(128)S(1)} %get-tuple-element.7, ...), channel_id=1, replica_groups=mesh['group'=2,'plane'=4,'planey'=2,'ens'=2] {'plane','planey'}, use_global_device_ids=true, to_apply=%region_8.9 | all-reduce | flops 8 | bytes 64 | tf_op jit(solution)/shard_map/psum | solution.py:151
  113.3 0.3 fusion.184
  113.6 2.0 %all-gather = f32[4,10,16,128]{3,2,1,0:T(8,128)S(1)} all-gather(f32[2,10,16,128]{3,2,1,0:T(8,128)S(1)} %fusion.184), channel_id=2, replica_groups=mesh['group'=2,'plane'=4,'planey'=2,'ens'=2] {'ens'}, dimensions={0}, use_global_device_ids=true | all-gather | bytes 491520 | tf_op jit(solution)/shard_map/all_gather | solution.py:176
  115.6 0.7 broadcast_multiply_fusion.3
  (27 shorter events, 0.2 us)
Async XLA Ops:
  0.7 20.2 %collective-permute-start.4 = (f32[1,1,1,4,128]{4,3,2,1,0:T(4,128)S(1)}, f32[1,1,1,4,128]{4,3,2,1,0:T(4,128)S(1)}, u32[]{:S(2)}, u32[]{:S(2)}) collective-permute-start(f32[1,1,1,4,128]{4,3,2,1,0:T(4,128)S(1)} %get-tuple-element.72), channel_id=1, source_target_pairs={{0,4},{4,8},{8,12},{1,5},{5,9},{9,13},{2,6},{6,10},{10,14},{3,7},{... | collective-permute-start | bytes 6152 | tf_op jit(solution)/shard_map/ppermute | solution.py:19
  5.7 16.5 %collective-permute-start.5 = (f32[1,1,1,4,128]{4,3,2,1,0:T(4,128)S(1)}, f32[1,1,1,4,128]{4,3,2,1,0:T(4,128)S(1)}, u32[]{:S(2)}, u32[]{:S(2)}) collective-permute-start(f32[1,1,1,4,128]{4,3,2,1,0:T(4,128)S(1)} %get-tuple-element.73), channel_id=1, source_target_pairs={{4,0},{8,4},{12,8},{5,1},{9,5},{13,9},{6,2},{10,6},{14,10},{7,3},{... | collective-permute-start | bytes 6152 | tf_op jit(solution)/shard_map/ppermute | solution.py:21
  7.7 19.2 %collective-permute-start.8 = (f32[1,1,1,4,128]{4,3,2,1,0:T(4,128)S(1)}, f32[1,1,1,4,128]{4,3,2,1,0:T(4,128)S(1)}, u32[]{:S(2)}, u32[]{:S(2)}) collective-permute-start(f32[1,1,1,4,128]{4,3,2,1,0:T(4,128)S(1)} %get-tuple-element.70), channel_id=1, source_target_pairs={{0,4},{4,8},{8,12},{1,5},{5,9},{9,13},{2,6},{6,10},{10,14},{3,7},{... | collective-permute-start | bytes 6152 | tf_op jit(solution)/shard_map/ppermute | solution.py:19
  12.2 18.0 %collective-permute-start.9 = (f32[1,1,1,4,128]{4,3,2,1,0:T(4,128)S(1)}, f32[1,1,1,4,128]{4,3,2,1,0:T(4,128)S(1)}, u32[]{:S(2)}, u32[]{:S(2)}) collective-permute-start(f32[1,1,1,4,128]{4,3,2,1,0:T(4,128)S(1)} %get-tuple-element.71), channel_id=1, source_target_pairs={{4,0},{8,4},{12,8},{5,1},{9,5},{13,9},{6,2},{10,6},{14,10},{7,3},{... | collective-permute-start | bytes 6152 | tf_op jit(solution)/shard_map/ppermute | solution.py:21
  15.3 26.8 %collective-permute-start.12 = (f32[2,1,1,4,128]{4,3,0,2,1:T(4,128)S(1)}, f32[2,1,1,4,128]{4,3,0,2,1:T(4,128)S(1)}, u32[]{:S(2)}, u32[]{:S(2)}) collective-permute-start(f32[2,1,1,4,128]{4,3,0,2,1:T(4,128)S(1)} %get-tuple-element.64), channel_id=1, source_target_pairs={{0,4},{4,8},{8,12},{1,5},{5,9},{9,13},{2,6},{6,10},{10,14},{3,7},{... | collective-permute-start | bytes 12296 | tf_op jit(solution)/shard_map/ppermute | solution.py:19
  20.9 21.2 %collective-permute-start.13 = (f32[2,1,1,4,128]{4,3,0,2,1:T(4,128)S(1)}, f32[2,1,1,4,128]{4,3,0,2,1:T(4,128)S(1)}, u32[]{:S(2)}, u32[]{:S(2)}) collective-permute-start(f32[2,1,1,4,128]{4,3,0,2,1:T(4,128)S(1)} %get-tuple-element.65), channel_id=1, source_target_pairs={{4,0},{8,4},{12,8},{5,1},{9,5},{13,9},{6,2},{10,6},{14,10},{7,3},{... | collective-permute-start | bytes 12296 | tf_op jit(solution)/shard_map/ppermute | solution.py:21
  22.2 27.9 %collective-permute-start = (f32[2,2,10,4,128]{4,3,2,1,0:T(4,128)S(1)}, f32[2,2,10,4,128]{4,3,2,1,0:T(4,128)S(1)}, u32[]{:S(2)}, u32[]{:S(2)}) collective-permute-start(f32[2,2,10,4,128]{4,3,2,1,0:T(4,128)S(1)} %get-tuple-element.56), channel_id=1, source_target_pairs={{0,4},{4,8},{8,12},{1,5},{5,9},{9,13},{2,6},{6,10},{10,14},{3,7},{... | collective-permute-start | bytes 245768 | tf_op jit(solution)/shard_map/ppermute | solution.py:19
  26.9 4.8 %collective-permute-start.6 = (f32[1,1,1,24,4]{4,3,2,1,0:T(8,128)S(1)}, f32[1,1,1,24,4]{4,3,2,1,0:T(8,128)S(1)}, u32[]{:S(2)}, u32[]{:S(2)}) collective-permute-start(f32[1,1,1,24,4]{4,3,2,1,0:T(8,128)S(1)} %get-tuple-element.68), channel_id=1, source_target_pairs={{0,2},{1,3},{4,6},{5,7},{8,10},{9,11},{12,14},{13,15},{16,18},{17,... | collective-permute-start | bytes 1160 | tf_op jit(solution)/shard_map/ppermute | solution.py:19
  30.3 5.9 %collective-permute-start.7 = (f32[1,1,1,24,4]{4,3,2,1,0:T(8,128)S(1)}, f32[1,1,1,24,4]{4,3,2,1,0:T(8,128)S(1)}, u32[]{:S(2)}, u32[]{:S(2)}) collective-permute-start(f32[1,1,1,24,4]{4,3,2,1,0:T(8,128)S(1)} %get-tuple-element.69), channel_id=1, source_target_pairs={{2,0},{3,1},{6,4},{7,5},{10,8},{11,9},{14,12},{15,13},{18,16},{19,... | collective-permute-start | bytes 1160 | tf_op jit(solution)/shard_map/ppermute | solution.py:21
  31.7 5.9 %collective-permute-start.10 = (f32[1,1,1,24,4]{4,3,2,1,0:T(8,128)S(1)}, f32[1,1,1,24,4]{4,3,2,1,0:T(8,128)S(1)}, u32[]{:S(2)}, u32[]{:S(2)}) collective-permute-start(f32[1,1,1,24,4]{4,3,2,1,0:T(8,128)S(1)} %get-tuple-element.66), channel_id=1, source_target_pairs={{0,2},{1,3},{4,6},{5,7},{8,10},{9,11},{12,14},{13,15},{16,18},{17,... | collective-permute-start | bytes 1160 | tf_op jit(solution)/shard_map/ppermute | solution.py:19
  36.2 5.6 %collective-permute-start.11 = (f32[1,1,1,24,4]{4,3,2,1,0:T(8,128)S(1)}, f32[1,1,1,24,4]{4,3,2,1,0:T(8,128)S(1)}, u32[]{:S(2)}, u32[]{:S(2)}) collective-permute-start(f32[1,1,1,24,4]{4,3,2,1,0:T(8,128)S(1)} %get-tuple-element.67), channel_id=1, source_target_pairs={{2,0},{3,1},{6,4},{7,5},{10,8},{11,9},{14,12},{15,13},{18,16},{19,... | collective-permute-start | bytes 1160 | tf_op jit(solution)/shard_map/ppermute | solution.py:21
  37.6 12.5 %collective-permute-start.1 = (f32[2,2,10,4,128]{4,3,2,1,0:T(4,128)S(1)}, f32[2,2,10,4,128]{4,3,2,1,0:T(4,128)S(1)}, u32[]{:S(2)}, u32[]{:S(2)}) collective-permute-start(f32[2,2,10,4,128]{4,3,2,1,0:T(4,128)S(1)} %get-tuple-element.57), channel_id=1, source_target_pairs={{4,0},{8,4},{12,8},{5,1},{9,5},{13,9},{6,2},{10,6},{14,10},{7,3},{... | collective-permute-start | bytes 245768 | tf_op jit(solution)/shard_map/ppermute | solution.py:21
  42.2 3.2 %collective-permute-start.14 = (f32[2,1,1,24,4]{4,3,0,2,1:T(8,128)S(1)}, f32[2,1,1,24,4]{4,3,0,2,1:T(8,128)S(1)}, u32[]{:S(2)}, u32[]{:S(2)}) collective-permute-start(f32[2,1,1,24,4]{4,3,0,2,1:T(8,128)S(1)} %get-tuple-element.62), channel_id=1, source_target_pairs={{0,2},{1,3},{4,6},{5,7},{8,10},{9,11},{12,14},{13,15},{16,18},{17,... | collective-permute-start | bytes 2312 | tf_op jit(solution)/shard_map/ppermute | solution.py:19
  43.8 5.7 %collective-permute-start.15 = (f32[2,1,1,24,4]{4,3,0,2,1:T(8,128)S(1)}, f32[2,1,1,24,4]{4,3,0,2,1:T(8,128)S(1)}, u32[]{:S(2)}, u32[]{:S(2)}) collective-permute-start(f32[2,1,1,24,4]{4,3,0,2,1:T(8,128)S(1)} %get-tuple-element.63), channel_id=1, source_target_pairs={{2,0},{3,1},{6,4},{7,5},{10,8},{11,9},{14,12},{15,13},{18,16},{19,... | collective-permute-start | bytes 2312 | tf_op jit(solution)/shard_map/ppermute | solution.py:21
  49.7 1.0 copy-start
  50.9 8.0 %collective-permute-start.2 = (f32[2,2,10,24,4]{4,3,2,1,0:T(8,128)S(1)}, f32[2,2,10,24,4]{4,3,2,1,0:T(8,128)S(1)}, u32[]{:S(2)}, u32[]{:S(2)}) collective-permute-start(f32[2,2,10,24,4]{4,3,2,1,0:T(8,128)S(1)} %get-tuple-element.54), channel_id=1, source_target_pairs={{0,2},{1,3},{4,6},{5,7},{8,10},{9,11},{12,14},{13,15},{16,18},{17,... | collective-permute-start | bytes 46088 | tf_op jit(solution)/shard_map/ppermute | solution.py:19
  52.6 10.7 %collective-permute-start.3 = (f32[2,2,10,24,4]{4,3,2,1,0:T(8,128)S(1)}, f32[2,2,10,24,4]{4,3,2,1,0:T(8,128)S(1)}, u32[]{:S(2)}, u32[]{:S(2)}) collective-permute-start(f32[2,2,10,24,4]{4,3,2,1,0:T(8,128)S(1)} %get-tuple-element.55), channel_id=1, source_target_pairs={{2,0},{3,1},{6,4},{7,5},{10,8},{11,9},{14,12},{15,13},{18,16},{19,... | collective-permute-start | bytes 46088 | tf_op jit(solution)/shard_map/ppermute | solution.py:21
  75.1 0.7 copy-start.2
  75.1 0.7 copy-start.3
  75.1 0.7 copy-start.4
  75.1 0.7 copy-start.5
  84.7 5.9 %copy-start.1 = (f32[2,10,16,128]{3,2,1,0:T(8,128)S(1)}, f32[2,10,16,128]{3,2,1,0:T(8,128)}, u32[]{:S(2)}) copy-start(f32[2,10,16,128]{3,2,1,0:T(8,128)} %slice_bitcast_fusion.8) | copy-start | bytes 491524
